TPU v7x, 32 devices: a whole 2x2x4 slice. The times are simulated.
32 devices in a mesh: band: 8 (over y, x, core), gblk: 4 (over z).
Axes of the slice: x: 2, y: 2, z: 4, core: 2. Of those that a mesh axis runs over, the one named last changes fastest.
Arguments:
- eps_inv: bfloat16 [2, 2, 8, 4, 512, 16384], P(None, None, None, 'gblk', None, 'band'), may hold values from -6 to 6
- pair_elements: bfloat16 [2, 1, 16, 16384], P(None, None, 'band'), may hold values from -0.046875 to 0.046875
Outputs:
- sigma_terms: float32 [2, 2, 1, 16], P(None, None, None, 'band')
All inputs are finite; a program needn't handle non-finite values.
Results may differ from a plain program's by a relative error of at most 0.0003.
Values may be sent and summed in bfloat16 or wider, within the bound.
A program may use at most 128 MiB of HBM per device.

v0:
```python
import jax
import jax.numpy as jnp
from jax import lax
from jax.sharding import PartitionSpec as P


def shards(eps_inv, pair_elements):
    group_count = lax.axis_size("gblk")
    group_index = lax.axis_index("gblk")
    freqs = eps_inv.shape[0]
    rounds = eps_inv.shape[2]
    tile_rows = eps_inv.shape[4]
    width = eps_inv.shape[5]
    states = pair_elements.shape[1]
    local_bands = pair_elements.shape[2]
    columns = lax.all_to_all(pair_elements, "band", split_axis=3, concat_axis=2, tiled=True)
    all_bands = columns.shape[2]
    blocks = eps_inv.reshape(freqs, 2, -1, width)
    shaped = pair_elements.reshape(2, states, local_bands, rounds, group_count, tile_rows)
    picked = lax.dynamic_slice_in_dim(shaped, group_index, 1, 4)
    row_local = picked.reshape(2, states, local_bands, rounds * tile_rows)
    flat = columns.reshape(-1, width)
    contract_last = (((1,), (1,)), ((), ()))
    images = []
    for frequency in range(freqs):
        along_a = lax.dot_general(
            flat, blocks[frequency, 0], contract_last, preferred_element_type=jnp.float32
        )
        along_b = lax.dot_general(
            flat, blocks[frequency, 1], contract_last, preferred_element_type=jnp.float32
        )
        along_a = along_a.reshape(2, states, all_bands, -1)
        along_b = along_b.reshape(2, states, all_bands, -1)
        images.append(jnp.stack([along_a[0] - along_b[1], along_a[1] + along_b[0]]))
    image = jnp.stack(images)
    piece = lax.all_gather(row_local, "band", axis=2, tiled=True)
    real_part = piece[0].astype(jnp.float32)
    imag_part = piece[1].astype(jnp.float32)
    sigma_re = jnp.sum(real_part * image[:, 0] + imag_part * image[:, 1], axis=-1)
    sigma_im = jnp.sum(real_part * image[:, 1] - imag_part * image[:, 0], axis=-1)
    partial_sigma = jnp.stack([sigma_re, sigma_im], axis=1)
    reduced = lax.psum_scatter(partial_sigma, "band", scatter_dimension=3, tiled=True)
    return lax.psum(reduced, "gblk")


def solution(mesh):
    placed = (P(None, None, None, "gblk", None, "band"), P(None, None, "band", None))
    return jax.shard_map(
        shards, mesh=mesh, in_specs=placed, out_specs=P(None, None, None, "band"), check_vma=False
    )
```

profile of v0, /device:TPU:0, one launch (start us, length us, event | category | flops | bytes accessed | tf_op | source)
XLA Modules:
  0.0 138.5 jit_solution(16395664978475546550)
XLA Ops:
  0.0 0.0 copy-start.1
  0.0 0.0 copy-start
  0.0 15.4 %copy.24 = bf16[2,1,2,16384]{2,0,1,3:T(2,128)(2,1)} copy(bf16[2,1,2,16384]{3,2,1,0:T(2,128)(2,1)} %param.3) | data formatting | bytes 262144 | tf_op args[1]
  15.5 13.7 %reshape.124 = bf16[8,2,4096]{2,1,0:T(2,128)(2,1)} reshape(bf16[16384,1,2,2]{3,2,1,0:T(2,128)(2,1)} %bitcast.63) | data formatting | bytes 262144
  29.2 5.2 %all-to-all-start = ((bf16[8,2,4096]{2,1,0:T(2,128)(2,1)}), bf16[8,2,4096]{2,1,0:T(2,128)(2,1)S(1)}, u32[]{:S(2)}, u32[]{:S(2)}) async-start(bf16[8,2,4096]{2,1,0:T(2,128)(2,1)} %reshape.124), calls=%async_computation | async-start | bytes 262144 | tf_op jit(solution)/shard_map/all_to_all | solution.py:16
  34.4 0.0 copy-done
  34.4 0.1 reshape.113
  34.5 0.2 dynamic-slice_reduce_fusion
  34.8 9.8 %all_gather.3 = bf16[2,1,16,4096]{3,0,1,2:T(2,128)(2,1)S(1)} all-gather(bf16[2,1,2,4096]{3,0,1,2:T(2,128)(2,1)S(1)} %copy.23), channel_id=1, replica_groups=mesh['band'=8,'gblk'=4] {'band'}, dimensions={2}, use_global_device_ids=true | all-gather | bytes 294912 | tf_op jit(solution)/shard_map/all_gather | solution.py:36
  44.6 0.5 slice_convert_fusion.1
  45.1 0.3 copy_bitcast_fusion
  45.4 0.0 copy-done.1
  45.4 0.6 dynamic-slice
  46.7 0.0 all-to-all-done
  46.7 19.1 %reshape.125 = bf16[16384,1,2,2]{3,2,1,0:T(2,128)(2,1)} reshape(bf16[8,2,4096]{2,1,0:T(2,128)(2,1)S(1)} %all-to-all-done) | data formatting | bytes 262144
  65.8 11.9 %copy.29 = bf16[2,1,2,8,2048]{4,3,2,0,1:T(8,128)(2,1)S(1)} copy(bf16[2,1,2,8,2048]{2,0,4,3,1:T(2,128)(2,1)} %bitcast.62) | data formatting | bytes 262144 | tf_op jit(solution)/shard_map/all_to_all | solution.py:16
  77.6 0.1 copy.26
  77.8 0.1 reshape.115
  77.9 8.6 %fusion.2 = f32[32,4096]{1,0:T(8,128)S(1)} fusion(bf16[32,2048]{1,0:T(8,128)(2,1)S(1)} %reshape.115, bf16[2,2,4096,2048]{3,2,1,0:T(8,128)(2,1)} %bitcast.2), kind=kOutput, calls=%fused_computation.5 | convolution fusion | flops 536870912 | bytes 17432576 | tf_op jit(solution)/shard_map/dot_general | solution.py:29
  86.4 8.6 %fusion.3 = f32[32,4096]{1,0:T(8,128)S(1)} fusion(bf16[32,2048]{1,0:T(8,128)(2,1)S(1)} %reshape.115, bf16[2,2,4096,2048]{3,2,1,0:T(8,128)(2,1)} %bitcast.2), kind=kOutput, calls=%fused_computation.7 | convolution fusion | flops 536870912 | bytes 17432576 | tf_op jit(solution)/shard_map/dot_general | solution.py:26
  95.0 8.6 %fusion = f32[32,4096]{1,0:T(8,128)S(1)} fusion(bf16[32,2048]{1,0:T(8,128)(2,1)S(1)} %reshape.115, bf16[2,2,4096,2048]{3,2,1,0:T(8,128)(2,1)} %bitcast.2), kind=kOutput, calls=%fused_computation.1 | convolution fusion | flops 536870912 | bytes 17432576 | tf_op jit(solution)/shard_map/dot_general | solution.py:29
  103.6 8.6 %fusion.1 = f32[32,4096]{1,0:T(8,128)S(1)} fusion(bf16[32,2048]{1,0:T(8,128)(2,1)S(1)} %reshape.115, bf16[2,2,4096,2048]{3,2,1,0:T(8,128)(2,1)} %bitcast.2), kind=kOutput, calls=%fused_computation.3 | convolution fusion | flops 536870912 | bytes 17432576 | tf_op jit(solution)/shard_map/dot_general | solution.py:26
  112.2 0.1 fusion.10
  112.3 0.1 fusion.8
  112.4 0.2 add_reduce_fusion
  112.7 13.2 %all-reduce = f32[2,2,1,16]{3,0,2,1:T(2,128)S(1)} all-reduce(f32[2,2,1,16]{3,0,2,1:T(2,128)S(1)} %pad_maximum_fusion.1), channel_id=2, replica_groups=mesh['band'=8,'gblk'=4] {'band'}, use_global_device_ids=true, to_apply=%region_2.0.clone | all-reduce | flops 64 | bytes 512
  125.9 0.1 constant_dynamic-slice_fusion
  125.9 11.9 %psum.7 = f32[2,2,1,2]{3,0,2,1:T(2,128)S(1)} all-reduce(f32[2,2,1,2]{3,0,2,1:T(2,128)S(1)} %constant_dynamic-slice_fusion), channel_id=1, replica_groups=mesh['band'=8,'gblk'=4] {'gblk'}, use_global_device_ids=true, to_apply=%region_3.0 | all-reduce | flops 8 | bytes 64 | tf_op jit(solution)/shard_map/psum | solution.py:43
  137.9 0.6 copy.28
  (5 shorter events, 0.1 us)
Async XLA Ops:
  0.0 45.4 %copy-start.1 = (u32[32]{0:T(128)S(1)}, u32[32]{0:T(128)}, u32[]{:S(2)}) copy-start(u32[32]{0:T(128)} %constant.14) | copy-start | bytes 388
  0.0 34.4 %copy-start = (bf16[2,1,2,16384]{3,2,1,0:T(2,128)(2,1)S(1)}, bf16[2,1,2,16384]{3,2,1,0:T(2,128)(2,1)}, u32[]{:S(2)}) copy-start(bf16[2,1,2,16384]{3,2,1,0:T(2,128)(2,1)} %param.3) | copy-start | bytes 393220
  29.2 17.5 %all-to-all-start = ((bf16[8,2,4096]{2,1,0:T(2,128)(2,1)}), bf16[8,2,4096]{2,1,0:T(2,128)(2,1)S(1)}, u32[]{:S(2)}, u32[]{:S(2)}) async-start(bf16[8,2,4096]{2,1,0:T(2,128)(2,1)} %reshape.124), calls=%async_computation | async-start | bytes 262144 | tf_op jit(solution)/shard_map/all_to_all | solution.py:16
where the time goes:
time: 140 us; the launch traced here: 138 us
  local copies, waits for them, and re-layouts  62.2 us (44%)
  blocking collectives  35 us (25%)
  matrix products  34.3 us (24%)
  starting transfers between devices  5.2 us (4%)
    unnamed x10, local copies, waits for them, and re-layouts  49.2 us
    dot_general x2, matrix products, shards(): lax.dot_general(flat, blocks[frequency, 0], contract_last, preferred_elem...  17.2 us
    dot_general x2, matrix products, shards(): lax.dot_general(flat, blocks[frequency, 1], contract_last, preferred_elem...  17.1 us
    unnamed x1, blocking collectives  13.2 us
    all_to_all x2, local copies, waits for them, and re-layouts, shards(): lax.all_to_all(pair_elements, 'band', split_axis=3, concat_axis=2, tiled=...  12 us
    psum x1, blocking collectives, shards(): return lax.psum(reduced, 'gblk')  11.9 us
    all_gather x1, blocking collectives, shards(): piece = lax.all_gather(row_local, 'band', axis=2, tiled=True)  9.81 us
    all_to_all x1, starting transfers between devices, shards(): lax.all_to_all(pair_elements, 'band', split_axis=3, concat_axis=2, tiled=...  5.2 us
  transfers between devices with their start and end apart: 1, of which 0 were waited for; matrix products, arithmetic and copies ran while one was open for 1% of the time, Pallas kernels for 0%

commit v1 on v0

v1 whole, which is shorter than its diff:
```python
import functools

import jax
import jax.numpy as jnp
from jax import lax
from jax.experimental import pallas as pl
from jax.experimental.pallas import tpu as pltpu
from jax.sharding import PartitionSpec as P

MESH = pl.DeviceIdType.MESH
RING_BYTES = 40 * 1024 * 1024
LANES = 128


def kernel(
    n, groups, eps, pair, out,
    slots, pairs, rowbuf, colbuf, wide, lhs, cols, swapped, acc, part, got, total, gathered,
    slot_sem, row_local, local_sem, row_send, row_recv, col_send, col_recv, one_send, one_recv, two_send, two_recv,
):
    me = lax.axis_index("band")
    group = lax.axis_index("gblk")
    freqs, rounds, tile_rows, width = eps.shape[0], eps.shape[2], eps.shape[4], eps.shape[5]
    states, bands = pair.shape[1], pair.shape[2]
    own = states * bands
    per_freq = 2 * rounds
    chunks = freqs * per_freq
    ring = slots.shape[0]

    def fetch(index):
        f = index // per_freq
        c = (index // rounds) % 2
        r = index % rounds
        s = index % ring
        return pltpu.make_async_copy(eps.at[f, c, r, 0], slots.at[s], slot_sem.at[s])

    row_copies = []
    for r in range(rounds):
        first = pl.multiple_of((r * groups + group) * tile_rows, tile_rows)
        row_copies.append(
            pltpu.make_async_copy(
                pair.at[:, :, :, pl.ds(first, tile_rows)],
                rowbuf.at[0, :, :, :, pl.ds(r * tile_rows, tile_rows)],
                row_local.at[r],
            )
        )
    for copy in row_copies:
        copy.start()
    pair_copy = pltpu.make_async_copy(pair, pairs, local_sem.at[0])
    pair_copy.start()
    own_first = pl.multiple_of(me * width, width)
    col_copy = pltpu.make_async_copy(pair.at[:, :, :, pl.ds(own_first, width)], colbuf.at[0], local_sem.at[1])
    col_copy.start()
    for index in range(min(ring, chunks)):
        fetch(index).start()

    barrier = pltpu.get_barrier_semaphore()
    for k in range(1, n):
        pl.semaphore_signal(barrier, inc=1, device_id=(lax.rem(me + k, n), group), device_id_type=MESH)
    for k in range(1, groups):
        pl.semaphore_signal(barrier, inc=1, device_id=(me, lax.rem(group + k, groups)), device_id_type=MESH)
    acc[...] = jnp.zeros_like(acc)
    for copy in row_copies:
        copy.wait()
    pair_copy.wait()
    col_copy.wait()
    pl.semaphore_wait(barrier, n + groups - 2)

    row_sends, col_sends = [], []
    for k in range(1, n):
        copy = pltpu.make_async_remote_copy(
            src_ref=rowbuf.at[0], dst_ref=rowbuf.at[k], send_sem=row_send.at[k], recv_sem=row_recv.at[k],
            device_id=(lax.rem(me + k, n), group), device_id_type=MESH,
        )
        copy.start()
        row_sends.append(copy)
    for k in range(1, n):
        target = lax.rem(me + k, n)
        first = pl.multiple_of(target * width, width)
        copy = pltpu.make_async_remote_copy(
            src_ref=pairs.at[:, :, :, pl.ds(first, width)], dst_ref=colbuf.at[k],
            send_sem=col_send.at[k], recv_sem=col_recv.at[k],
            device_id=(target, group), device_id_type=MESH,
        )
        copy.start()
        col_sends.append(copy)

    def place(k):
        for j in range(2):
            for s in range(states):
                at = (2 * k + j) * own + s * bands
                wide[at:at + bands, :] = rowbuf[k, j, s].astype(jnp.float32)

    place(0)
    for k in range(1, n):
        row_sends[k - 1].wait_recv()
        place(k)
    for r in range(rounds):
        lhs[r] = wide[:, r * tile_rows:(r + 1) * tile_rows].astype(jnp.bfloat16)

    def place_columns(k):
        for j in range(2):
            for s in range(states):
                piece = colbuf[k, j, s].astype(jnp.float32)
                at = (2 * k + j) * own + s * bands
                cols[at:at + bands, :] = piece
                other = (2 * k + 1 - j) * own + s * bands
                swapped[other:other + bands, :] = piece if j == 0 else -piece

    one_copies = []
    for f in range(freqs):
        def step(i, carry):
            index = f * per_freq + i
            fetch(index).wait()
            c = i // rounds
            acc[f, c] += jnp.dot(lhs[i % rounds], slots[index % ring], preferred_element_type=jnp.float32)

            @pl.when(index + ring < chunks)
            def _():
                fetch(index + ring).start()

            return carry

        lax.fori_loop(0, per_freq, step, 0)
        if f == 0:
            place_columns(0)
            for k in range(1, n):
                col_sends[k - 1].wait_recv()
                place_columns(k)
        real = jnp.zeros((acc.shape[2], LANES), jnp.float32)
        imag = jnp.zeros((acc.shape[2], LANES), jnp.float32)
        for start in range(0, width, LANES):
            window = slice(start, start + LANES)
            x, y = acc[f, 0, :, window], acc[f, 1, :, window]
            c, d = cols[:, window], swapped[:, window]
            real += x * c + y * d
            imag += y * c - x * d
        for k in range(n):
            part[f, k, 0:2 * own, :] = real[2 * own * k:2 * own * (k + 1), :]
            part[f, k, 2 * own:4 * own, :] = imag[2 * own * k:2 * own * (k + 1), :]
        for k in range(1, n):
            copy = pltpu.make_async_remote_copy(
                src_ref=part.at[f, k], dst_ref=got.at[f, k], send_sem=one_send.at[f, k], recv_sem=one_recv.at[f, k],
                device_id=(lax.rem(me + n - k, n), group), device_id_type=MESH,
            )
            copy.start()
            one_copies.append(copy)

    for f in range(freqs):
        value = part[f, 0]
        for k in range(1, n):
            one_copies[f * (n - 1) + k - 1].wait_recv()
            value += got[f, k]
        total[f] = value
        gathered[group, f] = value
    two_copies = []
    for k in range(1, groups):
        copy = pltpu.make_async_remote_copy(
            src_ref=total, dst_ref=gathered.at[group], send_sem=two_send.at[k], recv_sem=two_recv.at[k],
            device_id=(me, lax.rem(group + k, groups)), device_id_type=MESH,
        )
        copy.start()
        two_copies.append(copy)
    for copy in two_copies:
        copy.wait_recv()
    lane = lax.broadcasted_iota(jnp.int32, (1, bands), 1)
    for f in range(freqs):
        value = gathered[0, f]
        for k in range(1, groups):
            value += gathered[k, f]
        sums = jnp.sum(value, axis=1, keepdims=True)
        for c in range(2):
            for s in range(states):
                row = jnp.zeros((1, bands), jnp.float32)
                for b in range(bands):
                    at = 2 * own * c + s * bands + b
                    row = jnp.where(lane == b, sums[at:at + 1, :] + sums[at + own:at + own + 1, :], row)
                out[f, c, s:s + 1, :] = row
    for copy in row_sends + col_sends + one_copies + two_copies:
        copy.wait_send()


def shards(n, groups, eps_inv, pair_elements):
    freqs, _, rounds, _, tile_rows, width = eps_inv.shape
    _, states, bands, length = pair_elements.shape
    own = states * bands
    rows = 2 * own * n
    ring = max(1, min(freqs * 2 * rounds, RING_BYTES // (tile_rows * width * 2)))
    dma = pltpu.SemaphoreType.DMA
    return pl.pallas_call(
        functools.partial(kernel, n, groups),
        out_shape=jax.ShapeDtypeStruct((freqs, 2, states, bands), jnp.float32),
        in_specs=[pl.BlockSpec(memory_space=pl.ANY)] * 2,
        out_specs=pl.BlockSpec(memory_space=pltpu.VMEM),
        scratch_shapes=[
            pltpu.VMEM((ring, tile_rows, width), jnp.bfloat16),
            pltpu.VMEM((2, states, bands, length), jnp.bfloat16),
            pltpu.VMEM((n, 2, states, bands, rounds * tile_rows), jnp.bfloat16),
            pltpu.VMEM((n, 2, states, bands, width), jnp.bfloat16),
            pltpu.VMEM((rows, rounds * tile_rows), jnp.float32),
            pltpu.VMEM((rounds, rows, tile_rows), jnp.bfloat16),
            pltpu.VMEM((rows, width), jnp.float32),
            pltpu.VMEM((rows, width), jnp.float32),
            pltpu.VMEM((freqs, 2, rows, width), jnp.float32),
            pltpu.VMEM((freqs, n, 4 * own, LANES), jnp.float32),
            pltpu.VMEM((freqs, n, 4 * own, LANES), jnp.float32),
            pltpu.VMEM((freqs, 4 * own, LANES), jnp.float32),
            pltpu.VMEM((groups, freqs, 4 * own, LANES), jnp.float32),
            dma((ring,)), dma((rounds,)), dma((2,)),
            dma((n,)), dma((n,)), dma((n,)), dma((n,)),
            dma((freqs, n)), dma((freqs, n)), dma((groups,)), dma((groups,)),
        ],
        compiler_params=pltpu.CompilerParams(
            collective_id=0, has_side_effects=True, vmem_limit_bytes=60 * 1024 * 1024
        ),
    )(eps_inv, pair_elements)


def solution(mesh):
    placed = (P(None, None, None, "gblk", None, "band"), P(None, None, "band", None))
    return jax.shard_map(
        functools.partial(shards, mesh.shape["band"], mesh.shape["gblk"]),
        mesh=mesh, in_specs=placed, out_specs=P(None, None, None, "band"), check_vma=False,
    )
```

time: 140 us -> 46.1 us (0.33)
  local copies, waits for them, and re-layouts: 62.2 us -> 1.26 us
  Pallas kernels: 0 us -> 44.6 us
  blocking collectives: 35 us -> 0 us
  matrix products: 34.3 us -> 0 us
  starting transfers between devices: 5.2 us -> 0 us
    unnamed x10 -> x1, local copies, waits for them, and re-layouts: 49.2 us -> 1.26 us
    pallas_call x0 -> x1, Pallas kernels: none -> 44.6 us  [shards(): pl.pallas_call(functools.partial(kernel, n, groups), out_shape=jax.ShapeD...]
    dot_general x4 -> x0, matrix products: 34.3 us -> none  [the longest x2 17.2 us: shards(): lax.dot_general(flat, blocks[frequency, 0], contract_last, preferred_elem...]
    unnamed x1 -> x0, blocking collectives: 13.2 us -> none
    all_to_all x2 -> x0, local copies, waits for them, and re-layouts: 12 us -> none  [shards(): lax.all_to_all(pair_elements, 'band', split_axis=3, concat_axis=2, tiled=...]
    psum x1 -> x0, blocking collectives: 11.9 us -> none  [shards(): return lax.psum(reduced, 'gblk')]
    all_gather x1 -> x0, blocking collectives: 9.81 us -> none  [shards(): piece = lax.all_gather(row_local, 'band', axis=2, tiled=True)]
    all_to_all x1 -> x0, starting transfers between devices: 5.2 us -> none  [shards(): lax.all_to_all(pair_elements, 'band', split_axis=3, concat_axis=2, tiled=...]
  transfers between devices with their start and end apart: 1 -> 0, of which waited for: 0 -> 0; matrix products, arithmetic and copies ran while one was open for 1% -> 0% of each run, Pallas kernels for 0% -> 0%
where the time goes in v1:
time: 46.1 us; the launch traced here: 45.9 us
  Pallas kernels  44.6 us (97%)
  local copies, waits for them, and re-layouts  1.26 us (3%)
    pallas_call x1, Pallas kernels, shards(): pl.pallas_call(functools.partial(kernel, n, groups), out_shape=jax.ShapeD...  44.6 us
    unnamed x1, local copies, waits for them, and re-layouts  1.26 us

profile of v1, /device:TPU:0, one launch (start us, length us, event | category | flops | bytes accessed | tf_op | source)
XLA Modules:
  0.0 45.9 jit_solution(8370676735613327737)
XLA Ops:
  0.0 44.6 %shard_map.28 = f32[2,2,1,2]{3,2,1,0:T(1,128)} custom-call(bf16[2,2,8,1,512,2048]{5,4,3,2,1,0:T(8,128)(2,1)} %eps.1, bf16[2,1,2,16384]{3,2,1,0:T(2,128)(2,1)} %pair.1), custom_call_target="tpu_custom_call" | custom-call | tf_op jit(solution)/shard_map/pallas_call | solution.py:189
  44.7 1.3 %copy.4 = f32[2,2,1,2]{3,2,1,0:T(1,128)} copy(f32[2,2,1,2]{3,2,1,0:T(1,128)} %shard_map.28) | data formatting | bytes 64

commit v2 on v1

v2 whole, which is shorter than its diff:
```python
import functools

import jax
import jax.numpy as jnp
from jax import lax
from jax.experimental import pallas as pl
from jax.experimental.pallas import tpu as pltpu
from jax.sharding import PartitionSpec as P

MESH = pl.DeviceIdType.MESH
RING_BYTES = 40 * 1024 * 1024
SPAN = 2
EARLY = 10
LANES = 128


def kernel(
    n, groups, eps, pair, out,
    slots, pairs, rowbuf, colbuf, wide, lhs, cols, swapped, acc, part, got,
    slot_sem, row_local, local_sem, row_send, row_recv, col_send, col_recv, one_send, one_recv,
):
    me = lax.axis_index("band")
    group = lax.axis_index("gblk")
    freqs, rounds, tile_rows, width = eps.shape[0], eps.shape[2], eps.shape[4], eps.shape[5]
    states, bands = pair.shape[1], pair.shape[2]
    own = states * bands
    span = slot_sem.shape[1]
    per_part = rounds // span
    per_freq = 2 * per_part
    chunks = freqs * per_freq
    ring = slots.shape[0]

    def fetch(index):
        f = index // per_freq
        c = (index // per_part) % 2
        r = (index % per_part) * span
        s = index % ring
        return [
            pltpu.make_async_copy(
                eps.at[f, c, r + h, 0], slots.at[s, pl.ds(h * tile_rows, tile_rows)], slot_sem.at[s, h]
            )
            for h in range(span)
        ]

    def begin(index):
        for copy in fetch(index):
            copy.start(priority=1)

    row_copies = []
    for r in range(rounds):
        first = pl.multiple_of((r * groups + group) * tile_rows, tile_rows)
        row_copies.append(
            pltpu.make_async_copy(
                pair.at[:, :, :, pl.ds(first, tile_rows)],
                rowbuf.at[0, :, :, :, pl.ds(r * tile_rows, tile_rows)],
                row_local.at[r],
            )
        )
    for copy in row_copies:
        copy.start()
    pair_copy = pltpu.make_async_copy(pair, pairs, local_sem.at[0])
    pair_copy.start()
    own_first = pl.multiple_of(me * width, width)
    col_copy = pltpu.make_async_copy(pair.at[:, :, :, pl.ds(own_first, width)], colbuf.at[0], local_sem.at[1])
    col_copy.start()
    first_batch = min(EARLY, ring)
    for index in range(first_batch):
        begin(index)

    barrier = pltpu.get_barrier_semaphore()
    others = [(k, g) for g in range(groups) for k in range(n) if (k, g) != (0, 0)]
    for k, g in others:
        there = (lax.rem(me + k, n), lax.rem(group + g, groups))
        pl.semaphore_signal(barrier, inc=1, device_id=there, device_id_type=MESH)
    acc[...] = jnp.zeros_like(acc)
    for copy in row_copies:
        copy.wait()
    pair_copy.wait()
    col_copy.wait()
    pl.semaphore_wait(barrier, len(others))

    row_sends, col_sends = [], []
    for k in range(1, n):
        copy = pltpu.make_async_remote_copy(
            src_ref=rowbuf.at[0], dst_ref=rowbuf.at[k], send_sem=row_send.at[k], recv_sem=row_recv.at[k],
            device_id=(lax.rem(me + k, n), group), device_id_type=MESH,
        )
        copy.start()
        row_sends.append(copy)
    for k in range(1, n):
        target = lax.rem(me + k, n)
        first = pl.multiple_of(target * width, width)
        copy = pltpu.make_async_remote_copy(
            src_ref=pairs.at[:, :, :, pl.ds(first, width)], dst_ref=colbuf.at[k],
            send_sem=col_send.at[k], recv_sem=col_recv.at[k],
            device_id=(target, group), device_id_type=MESH,
        )
        copy.start()
        col_sends.append(copy)
    for index in range(first_batch, ring):
        begin(index)

    def place(k):
        for j in range(2):
            for s in range(states):
                at = (2 * k + j) * own + s * bands
                wide[at:at + bands, :] = rowbuf[k, j, s].astype(jnp.float32)

    place(0)
    for k in range(1, n):
        row_sends[k - 1].wait_recv()
        place(k)
    depth = span * tile_rows
    for r in range(per_part):
        lhs[r] = wide[:, r * depth:(r + 1) * depth].astype(jnp.bfloat16)

    def place_columns(k):
        for j in range(2):
            for s in range(states):
                piece = colbuf[k, j, s].astype(jnp.float32)
                at = (2 * k + j) * own + s * bands
                cols[at:at + bands, :] = piece
                other = (2 * k + 1 - j) * own + s * bands
                swapped[other:other + bands, :] = piece if j == 0 else -piece

    one_copies = []
    for f in range(freqs):
        def step(i, carry):
            index = f * per_freq + i
            for copy in fetch(index):
                copy.wait()
            c = i // per_part
            acc[f, c] += jnp.dot(lhs[i % per_part], slots[index % ring], preferred_element_type=jnp.float32)

            @pl.when(index + ring < chunks)
            def _():
                begin(index + ring)

            return carry

        lax.fori_loop(0, per_freq, step, 0)
        if f == 0:
            place_columns(0)
            for k in range(1, n):
                col_sends[k - 1].wait_recv()
                place_columns(k)
        real = jnp.zeros((acc.shape[2], LANES), jnp.float32)
        imag = jnp.zeros((acc.shape[2], LANES), jnp.float32)
        for start in range(0, width, LANES):
            window = slice(start, start + LANES)
            x, y = acc[f, 0, :, window], acc[f, 1, :, window]
            c, d = cols[:, window], swapped[:, window]
            real += x * c + y * d
            imag += y * c - x * d
        shape = real.shape
        lane = lax.broadcasted_iota(jnp.int32, shape, 1)
        turn = lax.rem(lax.broadcasted_iota(jnp.int32, shape, 0), 2 * own)
        marked = jnp.where(lane == turn, jnp.sum(real, axis=1, keepdims=True), 0.0)
        marked += jnp.where(lane == turn + 2 * own, jnp.sum(imag, axis=1, keepdims=True), 0.0)
        for k in range(n):
            part[f, k] = jnp.sum(marked[2 * own * k:2 * own * (k + 1), :], axis=0, keepdims=True)
        place_of = me * groups + group
        got[f, place_of] = part[f, 0]
        for k, g in others:
            copy = pltpu.make_async_remote_copy(
                src_ref=part.at[f, k], dst_ref=got.at[f, place_of],
                send_sem=one_send.at[f, k * groups + g], recv_sem=one_recv.at[f, k * groups + g],
                device_id=(lax.rem(me + n - k, n), lax.rem(group + g, groups)), device_id_type=MESH,
            )
            copy.start()
            one_copies.append(copy)

    for copy in one_copies:
        copy.wait_recv()
    for f in range(freqs):
        value = got[f, 0]
        for k in range(1, n * groups):
            value += got[f, k]
        for c in range(2):
            for s in range(states):
                at = 2 * own * c + s * bands
                out[f, c, s:s + 1, :] = value[:, at:at + bands] + value[:, at + own:at + own + bands]
    for copy in row_sends + col_sends + one_copies:
        copy.wait_send()


def shards(n, groups, eps_inv, pair_elements):
    freqs, _, rounds, _, tile_rows, width = eps_inv.shape
    _, states, bands, length = pair_elements.shape
    own = states * bands
    rows = 2 * own * n
    span = SPAN if rounds % SPAN == 0 else 1
    depth = span * tile_rows
    ring = max(1, min(freqs * 2 * rounds // span, RING_BYTES // (depth * width * 2)))
    dma = pltpu.SemaphoreType.DMA
    return pl.pallas_call(
        functools.partial(kernel, n, groups),
        out_shape=jax.ShapeDtypeStruct((freqs, 2, states, bands), jnp.float32),
        in_specs=[pl.BlockSpec(memory_space=pl.ANY)] * 2,
        out_specs=pl.BlockSpec(memory_space=pltpu.VMEM),
        scratch_shapes=[
            pltpu.VMEM((ring, depth, width), jnp.bfloat16),
            pltpu.VMEM((2, states, bands, length), jnp.bfloat16),
            pltpu.VMEM((n, 2, states, bands, rounds * tile_rows), jnp.bfloat16),
            pltpu.VMEM((n, 2, states, bands, width), jnp.bfloat16),
            pltpu.VMEM((rows, rounds * tile_rows), jnp.float32),
            pltpu.VMEM((rounds // span, rows, depth), jnp.bfloat16),
            pltpu.VMEM((rows, width), jnp.float32),
            pltpu.VMEM((rows, width), jnp.float32),
            pltpu.VMEM((freqs, 2, rows, width), jnp.float32),
            pltpu.VMEM((freqs, n, 1, LANES), jnp.float32),
            pltpu.VMEM((freqs, n * groups, 1, LANES), jnp.float32),
            dma((ring, span)), dma((rounds,)), dma((2,)),
            dma((n,)), dma((n,)), dma((n,)), dma((n,)),
            dma((freqs, n * groups)), dma((freqs, n * groups)),
        ],
        compiler_params=pltpu.CompilerParams(
            collective_id=0, has_side_effects=True, vmem_limit_bytes=60 * 1024 * 1024
        ),
    )(eps_inv, pair_elements)


def solution(mesh):
    placed = (P(None, None, None, "gblk", None, "band"), P(None, None, "band", None))
    return jax.shard_map(
        functools.partial(shards, mesh.shape["band"], mesh.shape["gblk"]),
        mesh=mesh, in_specs=placed, out_specs=P(None, None, None, "band"), check_vma=False,
    )
```

time: 46.1 us -> 34.1 us (0.74)
  Pallas kernels: 44.6 us -> 32.7 us
    pallas_call x1, Pallas kernels: 44.6 us -> 32.7 us  [shards(): pl.pallas_call(functools.partial(kernel, n, groups), out_shape=jax.ShapeD...]
where the time goes in v2:
time: 34.1 us; the launch traced here: 34 us
  Pallas kernels  32.7 us (96%)
  local copies, waits for them, and re-layouts  1.26 us (4%)
    pallas_call x1, Pallas kernels, shards(): pl.pallas_call(functools.partial(kernel, n, groups), out_shape=jax.ShapeD...  32.7 us
    unnamed x1, local copies, waits for them, and re-layouts  1.26 us

profile of v2, /device:TPU:0, one launch (start us, length us, event | category | flops | bytes accessed | tf_op | source)
XLA Modules:
  0.0 34.0 jit_solution(3764959287343060950)
XLA Ops:
  0.0 32.7 %shard_map.28 = f32[2,2,1,2]{3,2,1,0:T(1,128)} custom-call(bf16[2,2,8,1,512,2048]{5,4,3,2,1,0:T(8,128)(2,1)} %eps.1, bf16[2,1,2,16384]{3,2,1,0:T(2,128)(2,1)} %pair.1), custom_call_target="tpu_custom_call" | custom-call | tf_op jit(solution)/shard_map/pallas_call | solution.py:196
  32.7 1.3 %copy.4 = f32[2,2,1,2]{3,2,1,0:T(1,128)} copy(f32[2,2,1,2]{3,2,1,0:T(1,128)} %shard_map.28) | data formatting | bytes 64
